TPU v7x, 32 devices: a whole 2x2x4 slice. The times are simulated.
32 devices in a mesh: rep: 8 (over y, x, core), tp: 4 (over z).
Axes of the slice: x: 2, y: 2, z: 4, core: 2. Of those that a mesh axis runs over, the one named last changes fastest.
Arguments:
- states: bfloat16 [4, 32, 8192], P(None, 'rep'), may hold values from -6 to 6
- norm_gain: float32 [8192], replicated, may hold values from 0.1 to 1.9
- w_query: bfloat16 [8192, 8192], P(('rep', 'tp')), may hold values from -0.0625 to 0.0625
- w_key: bfloat16 [8192, 1024], P(('rep', 'tp')), may hold values from -0.0625 to 0.0625
- w_value: bfloat16 [8192, 1024], P(('rep', 'tp')), may hold values from -0.0625 to 0.0625
- w_out: bfloat16 [8192, 8192], P(None, ('rep', 'tp')), may hold values from -0.0625 to 0.0625
- bias_query: bfloat16 [8192], P('tp'), may hold values from -4 to 4
- bias_key: bfloat16 [1024], P('tp'), may hold values from -4 to 4
- bias_value: bfloat16 [1024], P('tp'), may hold values from -4 to 4
- key_cache: bfloat16 [32, 8, 4096, 128], P('rep', 'tp'), may hold values from -120 to 120
- value_cache: bfloat16 [32, 8, 4096, 128], P('rep', 'tp'), may hold values from -6 to 6
- lengths: int32 [32], P('rep'), may hold values from 1 to 4096, as said below
Outputs:
- mixed: bfloat16 [4, 32, 8192], P(None, 'rep', 'tp')
Inputs may be any that keep to these rules, and one draw needn't show every extreme that they name: `lengths`: each row's number of live cached positions; some row has exactly 4096.
All inputs are finite; a program needn't handle non-finite values.
Results may differ from a plain program's by a relative error of at most 0.0084.
Values may be sent and summed in bfloat16 or wider, within the bound.
A program may use at most 128 MiB of HBM per device.

v0:
```python
import jax
import jax.numpy as jnp
from jax import lax
from jax.sharding import PartitionSpec as P

BLK = 512
THETA = 1000000.0
EPS = 1e-06


def rotate(vectors, positions, head_size):
    half = head_size // 2
    freqs = THETA ** (-jnp.arange(half, dtype=jnp.float32) * 2.0 / head_size)
    angles = positions.astype(jnp.float32)[..., None, None] * freqs
    first = vectors[..., :half]
    second = vectors[..., half:]
    cosine = jnp.cos(angles)
    sine = jnp.sin(angles)
    return jnp.concatenate(
        [first * cosine - second * sine, second * cosine + first * sine], axis=-1
    )


def absorb(carry, scores, valid, values):
    top, total, accum = carry
    scores = jnp.where(valid, scores, -1e30)
    fresh = jnp.maximum(top, jnp.max(scores, axis=-1))
    weights = jnp.where(valid, jnp.exp(scores - fresh[..., None]), 0.0)
    factor = jnp.exp(top - fresh)
    total = total * factor + jnp.sum(weights, axis=-1)
    accum = accum * factor[..., None] + jnp.einsum(
        "bkqc,bkch->bkqh", weights.astype(jnp.bfloat16), values, preferred_element_type=jnp.float32
    )
    return (fresh, total, accum)


def attend(query, new_keys, new_values, key_cache, value_cache, lengths):
    steps, rows, heads_q, head_size = query.shape
    heads_kv = key_cache.shape[1]
    group = heads_q // heads_kv
    count = steps * group
    scale = 1.0 / head_size**0.5
    grouped = query.reshape(steps, rows, heads_kv, group, head_size).transpose(1, 2, 0, 3, 4)
    grouped = grouped.reshape(rows, heads_kv, count, head_size)
    start_top = jnp.full((rows, heads_kv, count), -1e30, jnp.float32)
    start_total = jnp.zeros((rows, heads_kv, count), jnp.float32)
    start_accum = jnp.zeros((rows, heads_kv, count, head_size), jnp.float32)

    def visit(index, carry):
        start = index * BLK
        keys = lax.dynamic_slice_in_dim(key_cache, start, BLK, 2)
        values = lax.dynamic_slice_in_dim(value_cache, start, BLK, 2)
        scores = (
            jnp.einsum("bkqh,bkch->bkqc", grouped, keys, preferred_element_type=jnp.float32) * scale
        )
        place = start + jnp.arange(BLK, dtype=jnp.int32)
        valid = (place[None, :] < lengths[:, None])[:, None, None, :]
        return absorb(carry, scores, valid, values)

    bound = key_cache.shape[2] // BLK
    carry = lax.fori_loop(0, bound, visit, (start_top, start_total, start_accum))
    fresh_keys = new_keys.transpose(1, 2, 0, 3)
    fresh_values = new_values.transpose(1, 2, 0, 3)
    scores = (
        jnp.einsum("bkqh,bkjh->bkqj", grouped, fresh_keys, preferred_element_type=jnp.float32)
        * scale
    )
    rank = jnp.arange(count, dtype=jnp.int32) // group
    valid = (jnp.arange(steps, dtype=jnp.int32)[None, :] <= rank[:, None])[None, None, :, :]
    top, total, accum = absorb(carry, scores, valid, fresh_values)
    attended = accum / total[..., None]
    attended = attended.reshape(rows, heads_kv, steps, group, head_size).transpose(2, 0, 1, 3, 4)
    return attended.reshape(steps * rows, heads_q * head_size).astype(jnp.bfloat16)


def on_device(
    states,
    norm_gain,
    w_query,
    w_key,
    w_value,
    w_out,
    bias_query,
    bias_key,
    bias_value,
    key_cache,
    value_cache,
    lengths,
):
    steps, rows, width = states.shape
    head_size = key_cache.shape[3]
    query_rows, key_rows, value_rows = (
        lax.all_to_all(w_query, "tp", split_axis=1, concat_axis=0, tiled=True),
        lax.all_to_all(w_key, "tp", split_axis=1, concat_axis=0, tiled=True),
        lax.all_to_all(w_value, "tp", split_axis=1, concat_axis=0, tiled=True),
    )
    out_block = lax.all_to_all(w_out, "tp", split_axis=0, concat_axis=1, tiled=True)
    flat = states.reshape(steps * rows, width).astype(jnp.float32)
    factor = lax.rsqrt(jnp.mean(flat * flat, axis=-1, keepdims=True) + EPS)
    normed = (flat * factor * norm_gain).astype(jnp.bfloat16)
    local_width = query_rows.shape[1]
    kv_width = key_rows.shape[1]
    stacked = jnp.concatenate([query_rows, key_rows, value_rows], axis=1)
    spread = lax.all_to_all(normed, "rep", split_axis=1, concat_axis=0, tiled=True)
    joined = lax.psum_scatter(
        jnp.dot(spread, stacked, preferred_element_type=jnp.float32),
        "rep",
        scatter_dimension=0,
        tiled=True,
    )
    query = joined[:, :local_width]
    keys = joined[:, local_width : local_width + kv_width]
    values = joined[:, local_width + kv_width :]
    query = query + bias_query.astype(jnp.float32)
    keys = keys + bias_key.astype(jnp.float32)
    values = values + bias_value.astype(jnp.float32)
    positions = lengths[None, :] + jnp.arange(steps, dtype=jnp.int32)[:, None]
    query = rotate(
        query.reshape(steps, rows, local_width // head_size, head_size), positions, head_size
    ).astype(jnp.bfloat16)
    keys = rotate(
        keys.reshape(steps, rows, kv_width // head_size, head_size), positions, head_size
    ).astype(jnp.bfloat16)
    values = values.reshape(steps, rows, kv_width // head_size, head_size).astype(jnp.bfloat16)
    attended = attend(query, keys, values, key_cache, value_cache, lengths)
    pieces = jnp.dot(
        lax.all_gather(attended, "rep", axis=0, tiled=True),
        out_block,
        preferred_element_type=jnp.float32,
    )
    partial_value = lax.all_to_all(
        pieces.astype(jnp.bfloat16), "rep", split_axis=0, concat_axis=1, tiled=True
    ).astype(pieces.dtype)
    summed = lax.psum_scatter(
        partial_value.astype(jnp.bfloat16), "tp", scatter_dimension=1, tiled=True
    ).astype(jnp.float32)
    column = lax.axis_index("tp") * summed.shape[1]
    residual = lax.dynamic_slice_in_dim(flat, column, summed.shape[1], 1)
    return (residual + summed).astype(jnp.bfloat16).reshape(steps, rows, summed.shape[1])


def solution(mesh):
    return jax.shard_map(
        on_device,
        mesh=mesh,
        in_specs=(
            P(None, "rep", None),
            P(),
            P(("rep", "tp"), None),
            P(("rep", "tp"), None),
            P(("rep", "tp"), None),
            P(None, ("rep", "tp")),
            P("tp"),
            P("tp"),
            P("tp"),
            P("rep", "tp", None, None),
            P("rep", "tp", None, None),
            P("rep"),
        ),
        out_specs=P(None, "rep", "tp"),
        check_vma=False,
    )
```

profile of v0, /device:TPU:0, one launch (start us, length us, event | category | flops | bytes accessed | tf_op | source)
XLA Modules:
  0.0 342.6 jit_solution(18113901410279301556)
XLA Ops:
  10.7 5.2 %all-to-all-start = ((bf16[16,8,1024]{2,0,1:T(8,128)(2,1)}), bf16[16,8,1024]{2,0,1:T(8,128)(2,1)S(1)}, u32[]{:S(2)}, u32[]{:S(2)}) async-start(bf16[16,8,1024]{2,0,1:T(8,128)(2,1)} %copy.46), calls=%async_computation | async-start | bytes 524288 | tf_op jit(solution)/shard_map/all_to_all | solution.py:104
  15.9 2.0 copy.51
  18.0 4.9 %all-to-all-done = bf16[16,8,1024]{2,0,1:T(8,128)(2,1)S(1)} async-done(((bf16[16,8,1024]{2,0,1:T(8,128)(2,1)}), bf16[16,8,1024]{2,0,1:T(8,128)(2,1)S(1)}, u32[]{:S(2)}, u32[]{:S(2)}) %all-to-all-start) | async-done | bytes 262176 | tf_op jit(solution)/shard_map/all_to_all | solution.py:104
  22.8 4.9 %all-to-all-start.3 = ((bf16[256,4,256]{0,2,1:T(8,128)(2,1)}), bf16[256,4,256]{0,2,1:T(8,128)(2,1)S(1)}, u32[]{:S(2)}, u32[]{:S(2)}) async-start(bf16[256,4,256]{0,2,1:T(8,128)(2,1)} %bitcast.8), calls=%async_computation.3 | async-start | bytes 1048576 | tf_op jit(solution)/shard_map/all_to_all | solution.py:95
  28.7 12.9 %all-to-all-done.3 = bf16[256,4,256]{0,2,1:T(8,128)(2,1)S(1)} async-done(((bf16[256,4,256]{0,2,1:T(8,128)(2,1)}), bf16[256,4,256]{0,2,1:T(8,128)(2,1)S(1)}, u32[]{:S(2)}, u32[]{:S(2)}) %all-to-all-start.3) | async-done | bytes 524320 | tf_op jit(solution)/shard_map/all_to_all | solution.py:95
  41.6 3.5 %all-to-all-start.2 = ((bf16[256,4,256]{0,2,1:T(8,128)(2,1)}), bf16[256,4,256]{0,2,1:T(8,128)(2,1)S(1)}, u32[]{:S(2)}, u32[]{:S(2)}) async-start(bf16[256,4,256]{0,2,1:T(8,128)(2,1)} %bitcast.5), calls=%async_computation.2 | async-start | bytes 1048576 | tf_op jit(solution)/shard_map/all_to_all | solution.py:94
  45.1 6.4 %copy.47 = bf16[256,8192]{0,1:T(8,128)(2,1)} copy(bf16[256,8192]{1,0:T(8,128)(2,1)} %param.16) | data formatting | bytes 8388608 | tf_op args[2]
  51.5 7.6 %all-to-all-done.2 = bf16[256,4,256]{0,2,1:T(8,128)(2,1)S(1)} async-done(((bf16[256,4,256]{0,2,1:T(8,128)(2,1)}), bf16[256,4,256]{0,2,1:T(8,128)(2,1)S(1)}, u32[]{:S(2)}, u32[]{:S(2)}) %all-to-all-start.2) | async-done | bytes 524320 | tf_op jit(solution)/shard_map/all_to_all | solution.py:94
  59.1 98.4 %all_to_all.111 = bf16[256,4,2048]{0,2,1:T(8,128)(2,1)} all-to-all(bf16[256,4,2048]{0,2,1:T(8,128)(2,1)} %bitcast.65), channel_id=1, replica_groups=mesh['rep'=8,'tp'=4] {'tp'}, dimensions={1} | all-to-all | bytes 8388608 | tf_op jit(solution)/shard_map/all_to_all | solution.py:93
  157.5 4.8 %all-to-all-start.4 = ((bf16[4,2048,256]{2,1,0:T(8,128)(2,1)}), bf16[4,2048,256]{2,1,0:T(8,128)(2,1)}, u32[]{:S(2)}, u32[]{:S(2)}) async-start(bf16[4,2048,256]{2,1,0:T(8,128)(2,1)} %bitcast.66), calls=%async_computation.5 | async-start | bytes 8388608 | tf_op jit(solution)/shard_map/all_to_all | solution.py:97
  162.8 6.3 %copy.48 = bf16[4,256,2048]{2,1,0:T(8,128)(2,1)} copy(bf16[4,256,2048]{1,2,0:T(8,128)(2,1)} %bitcast.64) | data formatting | bytes 8388608 | tf_op jit(solution)/shard_map/all_to_all | solution.py:93
  169.1 4.2 %fusion.15 = f32[128,2560]{1,0:T(8,128)} fusion(bf16[128,1024]{1,0:T(8,128)(2,1)S(1)} %bitcast.77, bf16[1024,256]{1,0:T(8,128)(2,1)S(1)} %bitcast.75, bf16[1024,256]{1,0:T(8,128)(2,1)S(1)} %bitcast.76, bf16[1024,2048]{1,0:T(8,128)(2,1)} %bitcast.67), kind=kOutput, calls=%fused_computation.23 | convolution fusion | flops 686817280 | bytes 6815744 | tf_op jit(solution)/shard_map/dot_general | solution.py:106
  173.8 80.7 %all-to-all-done.4 = bf16[4,2048,256]{2,1,0:T(8,128)(2,1)} async-done(((bf16[4,2048,256]{2,1,0:T(8,128)(2,1)}), bf16[4,2048,256]{2,1,0:T(8,128)(2,1)}, u32[]{:S(2)}, u32[]{:S(2)}) %all-to-all-start.4) | async-done | bytes 4194336 | tf_op jit(solution)/shard_map/all_to_all | solution.py:97
  254.5 6.4 %copy.61 = bf16[2048,4,256]{0,2,1:T(8,128)(2,1)} copy(bf16[2048,4,256]{2,0,1:T(8,128)(2,1)} %bitcast.21) | data formatting | bytes 8388608 | tf_op jit(solution)/shard_map/all_to_all | solution.py:97
  262.9 29.9 %while.18 = (s32[]{:T(128)}, f32[4,2,32]{2,1,0:T(2,128)S(1)}, f32[4,2,32]{2,1,0:T(2,128)S(1)}, f32[4,2,32,128]{3,2,1,0:T(8,128)S(1)}, s32[4]{0:T(128)S(1)}, /*in...) while((s32[]{:T(128)}, f32[4,2,32]{2,1,0:T(2,128)S(1)}, ...), condition=%wide.region_5.6_spmd.clone, body=%wide.region_2.5_spmd.clone.sunk | while | flops 68390656 | bytes 4026571 | solution.py:61
  263.0 1.8 fusion.59
  265.1 1.6 convolution_add_fusion.3
  266.7 1.8 fusion.59
  268.8 1.6 convolution_add_fusion.3
  270.5 1.8 fusion.59
  272.5 1.6 convolution_add_fusion.3
  274.2 1.8 fusion.59
  278.0 1.8 fusion.59
  281.7 1.8 fusion.59
  283.7 1.6 convolution_add_fusion.3
  285.4 1.8 fusion.59
  287.5 1.6 convolution_add_fusion.3
  289.2 1.8 fusion.59
  293.4 9.5 %all_gather.3 = bf16[128,2048]{1,0:T(8,128)(2,1)S(1)} all-gather(bf16[16,2048]{1,0:T(8,128)(2,1)S(1)} %convert_element_type.94), channel_id=1, replica_groups=mesh['rep'=8,'tp'=4] {'rep'}, dimensions={0}, use_global_device_ids=true | all-gather | bytes 589824 | tf_op jit(solution)/shard_map/all_gather | solution.py:127
  303.0 3.7 %convolution_convert_fusion = bf16[128,1024]{1,0:T(8,128)(2,1)S(1)} fusion(bf16[128,2048]{1,0:T(8,128)(2,1)S(1)} %all_gather.3, bf16[2048,1024]{0,1:T(8,128)(2,1)} %bitcast.63), kind=kOutput, calls=%fused_computation.29 | convolution fusion | flops 537001984 | bytes 4980736 | tf_op jit(solution)/shard_map/dot_general | solution.py:126
  306.7 9.4 %all_to_all.112 = bf16[8,16,1024]{2,1,0:T(8,128)(2,1)S(1)} all-to-all(bf16[8,16,1024]{2,1,0:T(8,128)(2,1)S(1)} %bitcast.71), channel_id=1, replica_groups=mesh['rep'=8,'tp'=4] {'rep'}, dimensions={0} | all-to-all | bytes 524288 | tf_op jit(solution)/shard_map/all_to_all | solution.py:131
  316.9 17.3 %reduce-scatter.5.cloned.1.call-done = bf16[16,2048]{1,0:T(8,128)(2,1)} async-done(((bf16[16,8192]{1,0:T(8,128)(2,1)}), bf16[16,2048]{1,0:T(8,128)(2,1)}) %reduce-scatter.5.cloned.1.call-update) | async-done | bytes 65552 | tf_op jit(solution)/shard_map/reduce_scatter | solution.py:134
  (111 shorter events, 18.3 us)
Async XLA Ops:
  6.5 21.2 %copy-start.1 = (bf16[256,1024]{1,0:T(8,128)(2,1)S(1)}, bf16[256,1024]{1,0:T(8,128)(2,1)}, u32[]{:S(2)}) copy-start(bf16[256,1024]{1,0:T(8,128)(2,1)} %param.17) | copy-start | bytes 1572868
  10.7 12.1 %all-to-all-start = ((bf16[16,8,1024]{2,0,1:T(8,128)(2,1)}), bf16[16,8,1024]{2,0,1:T(8,128)(2,1)S(1)}, u32[]{:S(2)}, u32[]{:S(2)}) async-start(bf16[16,8,1024]{2,0,1:T(8,128)(2,1)} %copy.46), calls=%async_computation | async-start | bytes 524288 | tf_op jit(solution)/shard_map/all_to_all | solution.py:104
  22.8 18.8 %all-to-all-start.3 = ((bf16[256,4,256]{0,2,1:T(8,128)(2,1)}), bf16[256,4,256]{0,2,1:T(8,128)(2,1)S(1)}, u32[]{:S(2)}, u32[]{:S(2)}) async-start(bf16[256,4,256]{0,2,1:T(8,128)(2,1)} %bitcast.8), calls=%async_computation.3 | async-start | bytes 1048576 | tf_op jit(solution)/shard_map/all_to_all | solution.py:95
  41.6 17.5 %all-to-all-start.2 = ((bf16[256,4,256]{0,2,1:T(8,128)(2,1)}), bf16[256,4,256]{0,2,1:T(8,128)(2,1)S(1)}, u32[]{:S(2)}, u32[]{:S(2)}) async-start(bf16[256,4,256]{0,2,1:T(8,128)(2,1)} %bitcast.5), calls=%async_computation.2 | async-start | bytes 1048576 | tf_op jit(solution)/shard_map/all_to_all | solution.py:94
  157.5 97.0 %all-to-all-start.4 = ((bf16[4,2048,256]{2,1,0:T(8,128)(2,1)}), bf16[4,2048,256]{2,1,0:T(8,128)(2,1)}, u32[]{:S(2)}, u32[]{:S(2)}) async-start(bf16[4,2048,256]{2,1,0:T(8,128)(2,1)} %bitcast.66), calls=%async_computation.5 | async-start | bytes 8388608 | tf_op jit(solution)/shard_map/all_to_all | solution.py:97
  162.3 98.6 %reduce-scatter.3.cloned.1.call-start = ((), (), s32[]{:S(2)}) async-start(), calls=%async_computation.8 | async-start | bytes 1474560 | tf_op jit(solution)/shard_map/reduce_scatter | solution.py:105
  169.1 4.3 %copy-start.4 = (bf16[256]{0:T(256)(128)(2,1)S(1)}, bf16[256]{0:T(256)(128)(2,1)}, u32[]{:S(2)}) copy-start(bf16[256]{0:T(256)(128)(2,1)} %param.21) | copy-start | bytes 1540
  169.1 4.4 %copy-start.5 = (bf16[256]{0:T(256)(128)(2,1)S(1)}, bf16[256]{0:T(256)(128)(2,1)}, u32[]{:S(2)}) copy-start(bf16[256]{0:T(256)(128)(2,1)} %param.22) | copy-start | bytes 1540
  169.1 4.4 %copy-start.2 = (s32[4]{0:T(128)S(1)}, s32[4]{0:T(128)}, u32[]{:S(2)}) copy-start(s32[4]{0:T(128)} %param.25) | copy-start | bytes 52
  169.1 4.6 %copy-start.3 = (bf16[2048]{0:T(1024)(128)(2,1)S(1)}, bf16[2048]{0:T(1024)(128)(2,1)}, u32[]{:S(2)}) copy-start(bf16[2048]{0:T(1024)(128)(2,1)} %param.20) | copy-start | bytes 12292
  173.4 160.9 %reduce-scatter.5.cloned.1.call-start = ((), (), s32[]{:S(2)}) async-start(), calls=%async_computation.9 | async-start | bytes 327680 | tf_op jit(solution)/shard_map/reduce_scatter | solution.py:134
  292.8 24.1 %copy-start = (bf16[4,4,8192]{2,1,0:T(4,128)(2,1)S(1)}, bf16[4,4,8192]{2,1,0:T(4,128)(2,1)}, u32[]{:S(2)}) copy-start(bf16[4,4,8192]{2,1,0:T(4,128)(2,1)} %param.14) | copy-start | bytes 786436
Sparse Core Ops, SparseCore 0:
  173.5 37.2 reduce-scatter.2
  317.0 17.1 reduce-scatter.4
where the time goes:
time: 344 us; the launch traced here: 343 us
  waiting for transfers between devices  123 us (36%)
  blocking collectives  117 us (34%)
  matrix products  35.1 us (10%)
  local copies, waits for them, and re-layouts  27 us (8%)
  starting transfers between devices  18.5 us (5%)
  between operations  13.7 us (4%)
  other arithmetic  7.12 us (2%)
    all_to_all x1, blocking collectives, on_device(): lax.all_to_all(w_query, 'tp', split_axis=1, concat_axis=0, tiled=True)  98.4 us
    all_to_all x1, waiting for transfers between devices, on_device(): lax.all_to_all(w_out, 'tp', split_axis=0, concat_axis=1, tiled=True)  80.7 us
    reduce_scatter x1, waiting for transfers between devices, on_device(): lax.psum_scatter(partial_value.astype(jnp.bfloat16), 'tp', scatter_dimens...  17.3 us
    dot_general x8, matrix products, visit(): jnp.einsum('bkqh,bkch->bkqc', grouped, keys, preferred_element_type=jnp.f...  14.1 us
    all_to_all x1, waiting for transfers between devices, on_device(): lax.all_to_all(w_value, 'tp', split_axis=1, concat_axis=0, tiled=True)  12.9 us
    dot_general x9, matrix products, absorb(): jnp.einsum('bkqc,bkch->bkqh', weights.astype(jnp.bfloat16), values, prefe...  12.8 us
    all_gather x1, blocking collectives, on_device(): lax.all_gather(attended, 'rep', axis=0, tiled=True)  9.51 us
    unnamed x16, local copies, waits for them, and re-layouts  9.48 us
  transfers between devices with their start and end apart: 6, of which 5 were waited for; matrix products, arithmetic and copies ran while one was open for 8% of the time, Pallas kernels for 0%

commit v1 on v0

--- a/solution.py
+++ b/solution.py
@@ -6,6 +6,22 @@
 BLK = 512
 THETA = 1000000.0
 EPS = 1e-06
+
+
+def exchange_in_pairs(x, axis, split, join):
+    ways, here = (lax.axis_size(axis), lax.axis_index(axis))
+    width = x.shape[split] // ways
+    dims = list(x.shape)
+    dims[split] = width
+    height = dims[join]
+    dims[join] = height * ways
+    full = jnp.zeros(dims, x.dtype)
+    for mask in range(ways):
+        part = lax.dynamic_slice_in_dim(x, (here ^ mask) * width, width, axis=split)
+        if mask:
+            part = lax.ppermute(part, axis, [(d, d ^ mask) for d in range(ways)])
+        full = lax.dynamic_update_slice_in_dim(full, part, (here ^ mask) * height, axis=join)
+    return full
 
 
 def rotate(vectors, positions, head_size):
@@ -90,7 +106,7 @@
     steps, rows, width = states.shape
     head_size = key_cache.shape[3]
     query_rows, key_rows, value_rows = (
-        lax.all_to_all(w_query, "tp", split_axis=1, concat_axis=0, tiled=True),
+        exchange_in_pairs(w_query, "tp", 1, 0),
         lax.all_to_all(w_key, "tp", split_axis=1, concat_axis=0, tiled=True),
         lax.all_to_all(w_value, "tp", split_axis=1, concat_axis=0, tiled=True),
     )

time: 344 us -> 282 us (0.82)
  blocking collectives: 117 us -> 20.2 us
  waiting for transfers between devices: 123 us -> 143 us
  starting transfers between devices: 18.5 us -> 36.7 us
    all_to_all x1 -> x0, blocking collectives: 98.4 us -> none  [on_device(): lax.all_to_all(w_query, 'tp', split_axis=1, concat_axis=0, tiled=True)]
    all_to_all x1, waiting for transfers between devices: 80.7 us -> 17.4 us  [on_device(): lax.all_to_all(w_out, 'tp', split_axis=0, concat_axis=1, tiled=True)]
    all_to_all x1, waiting for transfers between devices: 12.9 us -> 69.7 us  [on_device(): lax.all_to_all(w_value, 'tp', split_axis=1, concat_axis=0, tiled=True)]
    reduce_scatter x1, waiting for transfers between devices: 0.01 us -> 33.1 us  [on_device(): lax.psum_scatter(jnp.dot(spread, stacked, preferred_element_type=jnp.floa...]
    all_to_all x1, starting transfers between devices: 4.83 us -> 15 us  [on_device(): lax.all_to_all(w_out, 'tp', split_axis=0, concat_axis=1, tiled=True)]
    ppermute x0 -> x3, starting transfers between devices: none -> 8.17 us  [exchange_in_pairs(): part = lax.ppermute(part, axis, [(d, d ^ mask) for d in range(ways)])]
    dynamic_update_slice x0 -> x3, local copies, waits for them, and re-layouts: none -> 6.98 us  [exchange_in_pairs(): lax.dynamic_update_slice_in_dim(full, part, (here ^ mask) * height, axis=...]
    all_to_all x1 -> x0, local copies, waits for them, and re-layouts: 6.31 us -> none  [on_device(): lax.all_to_all(w_query, 'tp', split_axis=1, concat_axis=0, tiled=True)]
  transfers between devices with their start and end apart: 6 -> 9, of which waited for: 5 -> 5; matrix products, arithmetic and copies ran while one was open for 8% -> 16% of each run, Pallas kernels for 0% -> 0%
where the time goes in v1:
time: 282 us; the launch traced here: 281 us
  waiting for transfers between devices  143 us (51%)
  starting transfers between devices  36.7 us (13%)
  matrix products  35 us (12%)
  local copies, waits for them, and re-layouts  25.6 us (9%)
  blocking collectives  20.2 us (7%)
  between operations  13.7 us (5%)
  other arithmetic  6.17 us (2%)
    all_to_all x1, waiting for transfers between devices, on_device(): lax.all_to_all(w_value, 'tp', split_axis=1, concat_axis=0, tiled=True)  69.7 us
    reduce_scatter x1, waiting for transfers between devices, on_device(): lax.psum_scatter(jnp.dot(spread, stacked, preferred_element_type=jnp.floa...  33.1 us
    reduce_scatter x1, waiting for transfers between devices, on_device(): lax.psum_scatter(partial_value.astype(jnp.bfloat16), 'tp', scatter_dimens...  18.6 us
    all_to_all x1, waiting for transfers between devices, on_device(): lax.all_to_all(w_out, 'tp', split_axis=0, concat_axis=1, tiled=True)  17.4 us
    all_to_all x1, starting transfers between devices, on_device(): lax.all_to_all(w_out, 'tp', split_axis=0, concat_axis=1, tiled=True)  15 us
    dot_general x8, matrix products, visit(): jnp.einsum('bkqh,bkch->bkqc', grouped, keys, preferred_element_type=jnp.f...  14.1 us
    dot_general x9, matrix products, absorb(): jnp.einsum('bkqc,bkch->bkqh', weights.astype(jnp.bfloat16), values, prefe...  12.8 us
    all_to_all x1, blocking collectives, on_device(): lax.all_to_all(pieces.astype(jnp.bfloat16), 'rep', split_axis=0, concat_a...  10.4 us
  transfers between devices with their start and end apart: 9, of which 5 were waited for; matrix products, arithmetic and copies ran while one was open for 16% of the time, Pallas kernels for 0%

profile of v1, /device:TPU:0, one launch (start us, length us, event | category | flops | bytes accessed | tf_op | source)
XLA Modules:
  0.0 280.7 jit_solution(8963953840081262903)
XLA Ops:
  6.5 2.1 copy.45
  8.6 6.3 %all-to-all-start.1 = ((bf16[256,4,256]{0,2,1:T(8,128)(2,1)}), bf16[256,4,256]{0,2,1:T(8,128)(2,1)S(1)}, u32[]{:S(2)}, u32[]{:S(2)}) async-start(bf16[256,4,256]{0,2,1:T(8,128)(2,1)} %bitcast.2), calls=%async_computation.1 | async-start | bytes 1048576 | tf_op jit(solution)/shard_map/all_to_all | solution.py:110
  17.1 1.9 constant_dynamic-slice_fusion
  19.1 2.0 copy-done.1
  21.0 2.0 collective-permute-start
  23.1 2.4 collective-permute-start.1
  26.4 4.0 %all-to-all-done.1 = bf16[256,4,256]{0,2,1:T(8,128)(2,1)S(1)} async-done(((bf16[256,4,256]{0,2,1:T(8,128)(2,1)}), bf16[256,4,256]{0,2,1:T(8,128)(2,1)S(1)}, u32[]{:S(2)}, u32[]{:S(2)}) %all-to-all-start.1) | async-done | bytes 524320 | tf_op jit(solution)/shard_map/all_to_all | solution.py:110
  30.4 3.5 %all-to-all-start.2 = ((bf16[256,4,256]{0,2,1:T(8,128)(2,1)}), bf16[256,4,256]{0,2,1:T(8,128)(2,1)S(1)}, u32[]{:S(2)}, u32[]{:S(2)}) async-start(bf16[256,4,256]{0,2,1:T(8,128)(2,1)} %bitcast.5), calls=%async_computation.2 | async-start | bytes 1048576 | tf_op jit(solution)/shard_map/all_to_all | solution.py:111
  33.9 3.8 %collective-permute-start.2 = (bf16[256,2048]{1,0:T(8,128)(2,1)S(1)}, bf16[256,2048]{1,0:T(8,128)(2,1)}, u32[]{:S(2)}, u32[]{:S(2)}) collective-permute-start(bf16[256,2048]{1,0:T(8,128)(2,1)S(1)} %get-tuple-element.198), channel_id=1, source_target_pairs={{0,3},{1,2},{2,1},{3,0},{4,7},{5,6},{6,5},{7,4},{8,11},{9,10},{10,... | collective-permute-start | bytes 3145736 | tf_op jit(solution)/shard_map/ppermute | solution.py:22
  39.4 69.7 %all-to-all-done.2 = bf16[256,4,256]{0,2,1:T(8,128)(2,1)S(1)} async-done(((bf16[256,4,256]{0,2,1:T(8,128)(2,1)}), bf16[256,4,256]{0,2,1:T(8,128)(2,1)S(1)}, u32[]{:S(2)}, u32[]{:S(2)}) %all-to-all-start.2) | async-done | bytes 524320 | tf_op jit(solution)/shard_map/all_to_all | solution.py:111
  109.1 3.7 %all-to-all-start = ((bf16[16,8,1024]{2,0,1:T(8,128)(2,1)}), bf16[16,8,1024]{2,0,1:T(8,128)(2,1)S(1)}, u32[]{:S(2)}, u32[]{:S(2)}) async-start(bf16[16,8,1024]{2,0,1:T(8,128)(2,1)} %copy.44), calls=%async_computation | async-start | bytes 524288 | tf_op jit(solution)/shard_map/all_to_all | solution.py:120
  113.1 2.3 constant_dynamic-update-slice_fusion.2
  115.4 2.3 constant_dynamic-update-slice_fusion.1
  117.7 2.3 constant_dynamic-update-slice_fusion
  120.0 4.1 %fusion.15 = f32[128,2560]{1,0:T(8,128)} fusion(bf16[128,1024]{1,0:T(8,128)(2,1)S(1)} %bitcast.71, bf16[1024,256]{1,0:T(8,128)(2,1)S(1)} %bitcast.70, bf16[1024,256]{1,0:T(8,128)(2,1)S(1)} %bitcast.69, bf16[1024,2048]{1,0:T(8,128)(2,1)} %constant_dynamic-update-slice_fusion), kind=kOutput, calls=%fused_computation.23 | convolution fusion | flops 686817280 | bytes 6815744 | tf_op jit(solution)/shard_map/dot_general | solution.py:122
  124.3 15.0 %all-to-all-start.3 = ((bf16[4,2048,256]{2,1,0:T(8,128)(2,1)}), bf16[4,2048,256]{2,1,0:T(8,128)(2,1)}, u32[]{:S(2)}, u32[]{:S(2)}) async-start(bf16[4,2048,256]{2,1,0:T(8,128)(2,1)} %bitcast.61), calls=%async_computation.4 | async-start | bytes 8388608 | tf_op jit(solution)/shard_map/all_to_all | solution.py:113
  139.6 33.1 %reduce-scatter.3.cloned.1.call-done = f32[16,2560]{1,0:T(8,128)} async-done(((f32[128,2560]{1,0:T(8,128)}), f32[16,2560]{1,0:T(8,128)}) %reduce-scatter.3.cloned.1.call-update) | async-done | bytes 163856 | tf_op jit(solution)/shard_map/reduce_scatter | solution.py:121
  173.9 29.9 %while.18 = (s32[]{:T(128)}, f32[4,2,32]{2,1,0:T(2,128)S(1)}, f32[4,2,32]{2,1,0:T(2,128)S(1)}, f32[4,2,32,128]{3,2,1,0:T(8,128)S(1)}, s32[4]{0:T(128)S(1)}, /*in...) while((s32[]{:T(128)}, f32[4,2,32]{2,1,0:T(2,128)S(1)}, ...), condition=%wide.region_5.6_spmd.clone, body=%wide.region_2.5_spmd.clone.sunk | while | flops 68390656 | bytes 4026571 | solution.py:77
  174.0 1.8 fusion.59
  177.7 1.8 fusion.59
  181.4 1.8 fusion.59
  185.2 1.8 fusion.59
  188.9 1.8 fusion.59
  192.7 1.8 fusion.59
  196.4 1.8 fusion.59
  200.1 1.8 fusion.59
  205.2 9.8 %all_gather.3 = bf16[128,2048]{1,0:T(8,128)(2,1)S(1)} all-gather(bf16[16,2048]{1,0:T(8,128)(2,1)S(1)} %convert_element_type.94), channel_id=1, replica_groups=mesh['rep'=8,'tp'=4] {'rep'}, dimensions={0}, use_global_device_ids=true | all-gather | bytes 589824 | tf_op jit(solution)/shard_map/all_gather | solution.py:143
  215.1 17.4 %all-to-all-done.3 = bf16[4,2048,256]{2,1,0:T(8,128)(2,1)} async-done(((bf16[4,2048,256]{2,1,0:T(8,128)(2,1)}), bf16[4,2048,256]{2,1,0:T(8,128)(2,1)}, u32[]{:S(2)}, u32[]{:S(2)}) %all-to-all-start.3) | async-done | bytes 4194336 | tf_op jit(solution)/shard_map/all_to_all | solution.py:113
  232.5 6.3 %copy.57 = bf16[2048,4,256]{0,2,1:T(8,128)(2,1)} copy(bf16[2048,4,256]{2,0,1:T(8,128)(2,1)} %bitcast.18) | data formatting | bytes 8388608 | tf_op jit(solution)/shard_map/all_to_all | solution.py:113
  238.8 3.7 %convolution_convert_fusion = bf16[128,1024]{1,0:T(8,128)(2,1)S(1)} fusion(bf16[128,2048]{1,0:T(8,128)(2,1)S(1)} %all_gather.3, bf16[2048,1024]{0,1:T(8,128)(2,1)} %bitcast.60), kind=kOutput, calls=%fused_computation.29 | convolution fusion | flops 537001984 | bytes 4980736 | tf_op jit(solution)/shard_map/dot_general | solution.py:142
  242.5 10.4 %all_to_all.92 = bf16[8,16,1024]{2,1,0:T(8,128)(2,1)S(1)} all-to-all(bf16[8,16,1024]{2,1,0:T(8,128)(2,1)S(1)} %bitcast.65), channel_id=1, replica_groups=mesh['rep'=8,'tp'=4] {'rep'}, dimensions={0} | all-to-all | bytes 524288 | tf_op jit(solution)/shard_map/all_to_all | solution.py:147
  253.7 18.6 %reduce-scatter.5.cloned.1.call-done = bf16[16,2048]{1,0:T(8,128)(2,1)} async-done(((bf16[16,8192]{1,0:T(8,128)(2,1)}), bf16[16,2048]{1,0:T(8,128)(2,1)}) %reduce-scatter.5.cloned.1.call-update) | async-done | bytes 65552 | tf_op jit(solution)/shard_map/reduce_scatter | solution.py:150
  (125 shorter events, 25.6 us)
Async XLA Ops:
  8.6 21.8 %all-to-all-start.1 = ((bf16[256,4,256]{0,2,1:T(8,128)(2,1)}), bf16[256,4,256]{0,2,1:T(8,128)(2,1)S(1)}, u32[]{:S(2)}, u32[]{:S(2)}) async-start(bf16[256,4,256]{0,2,1:T(8,128)(2,1)} %bitcast.2), calls=%async_computation.1 | async-start | bytes 1048576 | tf_op jit(solution)/shard_map/all_to_all | solution.py:110
  14.9 2.2 copy-start
  17.1 8.3 %copy-start.3 = (bf16[256,1024]{1,0:T(8,128)(2,1)S(1)}, bf16[256,1024]{1,0:T(8,128)(2,1)}, u32[]{:S(2)}) copy-start(bf16[256,1024]{1,0:T(8,128)(2,1)} %param.18) | copy-start | bytes 1572868
  17.1 20.6 %copy-start.2 = (bf16[4,4,8192]{2,1,0:T(4,128)(2,1)S(1)}, bf16[4,4,8192]{2,1,0:T(4,128)(2,1)}, u32[]{:S(2)}) copy-start(bf16[4,4,8192]{2,1,0:T(4,128)(2,1)} %param.14) | copy-start | bytes 786436
  17.1 20.7 %copy-start.4 = (f32[8192]{0:T(1024)S(1)}, f32[8192]{0:T(1024)}, u32[]{:S(2)}) copy-start(f32[8192]{0:T(1024)} %param.15) | copy-start | bytes 98308
  19.1 2.0 copy-start.1
  21.0 92.0 %collective-permute-start = (bf16[256,2048]{1,0:T(8,128)(2,1)}, bf16[256,2048]{1,0:T(8,128)(2,1)}, u32[]{:S(2)}, u32[]{:S(2)}) collective-permute-start(bf16[256,2048]{1,0:T(8,128)(2,1)} %get-tuple-element.199), channel_id=1, source_target_pairs={{0,1},{1,0},{2,3},{3,2},{4,5},{5,4},{6,7},{7,6},{8,9},{9,8},{10,11... | collective-permute-start | bytes 3145736 | tf_op jit(solution)/shard_map/ppermute | solution.py:22
  23.1 92.3 %collective-permute-start.1 = (bf16[256,2048]{1,0:T(8,128)(2,1)}, bf16[256,2048]{1,0:T(8,128)(2,1)}, u32[]{:S(2)}, u32[]{:S(2)}) collective-permute-start(bf16[256,2048]{1,0:T(8,128)(2,1)} %get-tuple-element.201), channel_id=1, source_target_pairs={{0,2},{1,3},{2,0},{3,1},{4,6},{5,7},{6,4},{7,5},{8,10},{9,11},{10,... | collective-permute-start | bytes 3145736 | tf_op jit(solution)/shard_map/ppermute | solution.py:22
  30.4 78.6 %all-to-all-start.2 = ((bf16[256,4,256]{0,2,1:T(8,128)(2,1)}), bf16[256,4,256]{0,2,1:T(8,128)(2,1)S(1)}, u32[]{:S(2)}, u32[]{:S(2)}) async-start(bf16[256,4,256]{0,2,1:T(8,128)(2,1)} %bitcast.5), calls=%async_computation.2 | async-start | bytes 1048576 | tf_op jit(solution)/shard_map/all_to_all | solution.py:111
  33.9 83.8 %collective-permute-start.2 = (bf16[256,2048]{1,0:T(8,128)(2,1)S(1)}, bf16[256,2048]{1,0:T(8,128)(2,1)}, u32[]{:S(2)}, u32[]{:S(2)}) collective-permute-start(bf16[256,2048]{1,0:T(8,128)(2,1)S(1)} %get-tuple-element.198), channel_id=1, source_target_pairs={{0,3},{1,2},{2,1},{3,0},{4,7},{5,6},{6,5},{7,4},{8,11},{9,10},{10,... | collective-permute-start | bytes 3145736 | tf_op jit(solution)/shard_map/ppermute | solution.py:22
  109.1 11.0 %all-to-all-start = ((bf16[16,8,1024]{2,0,1:T(8,128)(2,1)}), bf16[16,8,1024]{2,0,1:T(8,128)(2,1)S(1)}, u32[]{:S(2)}, u32[]{:S(2)}) async-start(bf16[16,8,1024]{2,0,1:T(8,128)(2,1)} %copy.44), calls=%async_computation | async-start | bytes 524288 | tf_op jit(solution)/shard_map/all_to_all | solution.py:120
  112.8 59.9 %reduce-scatter.3.cloned.1.call-start = ((), (), s32[]{:S(2)}) async-start(), calls=%async_computation.7 | async-start | bytes 1474560 | tf_op jit(solution)/shard_map/reduce_scatter | solution.py:121
  124.2 15.0 %copy-start.7 = (bf16[256]{0:T(256)(128)(2,1)S(1)}, bf16[256]{0:T(256)(128)(2,1)}, u32[]{:S(2)}) copy-start(bf16[256]{0:T(256)(128)(2,1)} %param.21) | copy-start | bytes 1540
  124.2 15.0 %copy-start.8 = (bf16[256]{0:T(256)(128)(2,1)S(1)}, bf16[256]{0:T(256)(128)(2,1)}, u32[]{:S(2)}) copy-start(bf16[256]{0:T(256)(128)(2,1)} %param.22) | copy-start | bytes 1540
  124.2 15.0 %copy-start.6 = (bf16[2048]{0:T(1024)(128)(2,1)S(1)}, bf16[2048]{0:T(1024)(128)(2,1)}, u32[]{:S(2)}) copy-start(bf16[2048]{0:T(1024)(128)(2,1)} %param.20) | copy-start | bytes 12292
  124.2 15.1 %copy-start.5 = (s32[4]{0:T(128)S(1)}, s32[4]{0:T(128)}, u32[]{:S(2)}) copy-start(s32[4]{0:T(128)} %param.25) | copy-start | bytes 52
  124.3 108.3 %all-to-all-start.3 = ((bf16[4,2048,256]{2,1,0:T(8,128)(2,1)}), bf16[4,2048,256]{2,1,0:T(8,128)(2,1)}, u32[]{:S(2)}, u32[]{:S(2)}) async-start(bf16[4,2048,256]{2,1,0:T(8,128)(2,1)} %bitcast.61), calls=%async_computation.4 | async-start | bytes 8388608 | tf_op jit(solution)/shard_map/all_to_all | solution.py:113
  139.2 133.1 %reduce-scatter.5.cloned.1.call-start = ((), (), s32[]{:S(2)}) async-start(), calls=%async_computation.8 | async-start | bytes 327680 | tf_op jit(solution)/shard_map/reduce_scatter | solution.py:150
Sparse Core Ops, SparseCore 0:
  124.3 48.3 reduce-scatter.2
  253.8 18.4 reduce-scatter.4
